TPU v7x, 32 devices: a whole 2x2x4 slice. The times are simulated.
32 devices in a mesh: row: 2 (over y), col: 8 (over z, x), rep: 2 (over core).
Axes of the slice: x: 2, y: 2, z: 4, core: 2. Of those that a mesh axis runs over, the one named last changes fastest.
Arguments:
- gain: float32 [48, 8, 128, 128], P(('row', 'col'), 'rep'), as said below
- coupled_columns: int32 [48, 8], P(('row', 'col')), may hold values from 0 to 47, as said below
- solution: float32 [6144, 512], P(('row', 'col')), may hold values from -6 to 6
- residual: float32 [6144, 512], P(('row', 'col')), may hold values from -6 to 6
- direction: float32 [6144, 512], P(('row', 'col')), may hold values from -6 to 6
Outputs:
- solution_next: float32 [6144, 512], P(('row', 'col'))
- residual_next: float32 [6144, 512], P(('row', 'col'))
- direction_next: float32 [6144, 512], P(('row', 'col'))
Inputs may be any that keep to these rules, and one draw needn't show every extreme that they name: `coupled_columns`: each block row i names first its coupled block columns in ascending order (always i - 1, i, i + 1 where inside 0 to 47, some of i - 3, i - 2, i + 2, i + 3, the coupling being symmetric), at most 7 of them, and then fills the remaining slots with i itself; every named column is within 3 of i. The gain matrix assembled from its blocks is symmetric; padding slots hold zero blocks; each diagonal entry exceeds the sum of the absolute values of the other entries of its row by exactly 1.
All inputs are finite; a program needn't handle non-finite values.
Results may differ from a plain program's by a relative error of at most 0.000061.
Values sent between devices are 32-bit elements; how exact they have to be, the bound alone decides.
A program may use at most 64 MiB of HBM per device.

v0:
```python
import jax
import jax.numpy as jnp
from jax import lax
from jax.sharding import PartitionSpec as P

BLK = 128


reach_blocks = 3


def extended_2(block, sides, width):
    for axis, dim in sides:
        count = lax.axis_size(axis)
        forward = [(i, i + 1) for i in range(count - 1)]
        backward = [(target, source) for source, target in forward]
        low = lax.ppermute(
            lax.slice_in_dim(block, block.shape[dim] - width, None, axis=dim), axis, forward
        )
        high = lax.ppermute(lax.slice_in_dim(block, 0, width, axis=dim), axis, backward)
        block = jnp.concatenate([low, block, high], axis=dim)
    return block


def per_device(gain, coupled_columns, solution, residual, direction):
    row_blocks = coupled_columns.shape[0]
    snapshots = direction.shape[1]
    first_block = lax.axis_index(("row", "col")) * row_blocks
    extended = extended_2(direction, ((("row", "col"), 0),), reach_blocks * BLK)
    segments = extended.reshape(row_blocks + 2 * reach_blocks, BLK, snapshots)
    half_slots = gain.shape[1]
    own_columns = lax.dynamic_slice_in_dim(
        coupled_columns, lax.axis_index("rep") * half_slots, half_slots, 1
    )
    local_index = own_columns - first_block + reach_blocks
    picked = segments[local_index]
    product = jnp.einsum(
        "rkab,rkbs->ras",
        gain,
        picked,
        precision=lax.Precision.HIGHEST,
        preferred_element_type=jnp.float32,
    )
    image = lax.psum(product.reshape(row_blocks * BLK, snapshots), "rep")
    norm_old, curvature, crossing, image_square = lax.psum(
        (
            jnp.sum(residual * residual, axis=0),
            jnp.sum(direction * image, axis=0),
            jnp.sum(residual * image, axis=0),
            jnp.sum(image * image, axis=0),
        ),
        ("row", "col"),
    )
    step_size = norm_old / curvature
    solution_next = solution + step_size * direction
    residual_next = residual - step_size * image
    norm_new = norm_old - 2.0 * step_size * crossing + step_size * step_size * image_square
    direction_next = residual_next + norm_new / norm_old * direction
    return (solution_next, residual_next, direction_next)


def solution(mesh):
    return jax.shard_map(
        per_device,
        mesh=mesh,
        in_specs=(
            P(("row", "col"), "rep", None, None),
            P(("row", "col"), None),
            P(("row", "col"), None),
            P(("row", "col"), None),
            P(("row", "col"), None),
        ),
        out_specs=(P(("row", "col"), None), P(("row", "col"), None), P(("row", "col"), None)),
        check_vma=False,
    )
```

profile of v0, /device:TPU:0, one launch (start us, length us, event | category | flops | bytes accessed | tf_op | source)
XLA Modules:
  0.0 132.4 jit_solution(13395826707546090617)
XLA Ops:
  7.2 0.0 copy-start
  7.2 0.0 all-reduce.3.cloned.1.call-start
  7.2 1.4 %collective-permute-start.1 = (f32[384,512]{1,0:T(8,128)}, f32[384,512]{1,0:T(8,128)S(1)}, u32[]{:S(2)}, u32[]{:S(2)}) collective-permute-start(f32[384,512]{1,0:T(8,128)} %param.9), channel_id=1, source_target_pairs={{2,0},{4,2},{6,4},{8,6},{10,8},{12,10},{14,12},{16,14},{18,16},{20... | collective-permute-start | bytes 2359304 | tf_op jit(solution)/shard_map/ppermute | solution.py:20
  8.7 6.4 %collective-permute-start = (f32[384,512]{1,0:T(8,128)}, f32[384,512]{1,0:T(8,128)}, u32[]{:S(2)}, u32[]{:S(2)}) collective-permute-start(f32[384,512]{1,0:T(8,128)} %param.9), channel_id=1, source_target_pairs={{0,2},{2,4},{4,6},{6,8},{8,10},{10,12},{12,14},{14,16},{16,18},{18... | collective-permute-start | bytes 2359304 | tf_op jit(solution)/shard_map/ppermute | solution.py:17
  15.0 0.8 compare_select_fusion
  15.8 0.1 reshape.18
  15.9 30.9 %collective-permute-done.1 = f32[384,512]{1,0:T(8,128)S(1)} collective-permute-done((f32[384,512]{1,0:T(8,128)}, f32[384,512]{1,0:T(8,128)S(1)}, u32[]{:S(2)}, u32[]{:S(2)}) %collective-permute-start.1) | collective-permute-done | bytes 786464 | tf_op jit(solution)/shard_map/ppermute | solution.py:20
  46.8 0.0 copy-start.4
  46.8 0.9 copy-done.4
  47.7 0.0 collective-permute-done
  47.7 1.8 %pad_maximum_fusion = f32[1152,512]{1,0:T(8,128)S(1)} fusion(f32[384,512]{1,0:T(8,128)} %copy-done.4, f32[384,512]{1,0:T(8,128)} %param.9, f32[384,512]{1,0:T(8,128)} %collective-permute-done), kind=kLoop, calls=%fused_computation.1 | loop fusion | flops 1179648 | bytes 4718592 | tf_op jit(solution)/shard_map/concatenate | solution.py:21
  49.5 2.4 %gather_fusion = f32[12,128,512]{2,1,0:T(8,128)} fusion(f32[9,128,512]{2,1,0:T(8,128)S(1)} %bitcast.10, s32[1024]{0:T(1024)S(1)} %pad_clamp_fusion), kind=kCustom, calls=%fused_computation | custom fusion | bytes 6291504 | tf_op jit(solution)/shard_map/gather | solution.py:36
  51.9 0.0 copy-start.1
  51.9 0.0 copy-start.2
  51.9 0.0 copy-done
  52.0 0.0 copy-start.3
  52.0 4.8 %fusion = f32[3,512,128,1]{1,2,3,0:T(8,128)} fusion(f32[3,4,128,512]{3,2,1,0:T(8,128)} %bitcast.11, f32[3,4,128,128]{3,2,1,0:T(8,128)S(1)} %copy-done), kind=kOutput, calls=%fused_computation.12 | convolution fusion | flops 1207959552 | bytes 4718592 | tf_op jit(solution)/shard_map/rkab,rkbs->ras/dot_general | solution.py:37
  56.7 0.0 all-reduce.3.cloned.1.call-update
  56.7 22.1 %all-reduce.3.cloned.1.call-done = f32[384,512]{1,0:T(8,128)} async-done(((f32[384,512]{1,0:T(8,128)}), f32[384,512]{1,0:T(8,128)}) %all-reduce.3.cloned.1.call-update) | async-done | bytes 786448 | tf_op jit(solution)/shard_map/psum | solution.py:44
  78.8 0.0 copy-done.1
  78.8 0.0 copy-done.2
  78.8 1.4 %multiply_reduce_fusion.1 = (f32[512]{0:T(512)S(1)}, f32[512]{0:T(512)S(1)}, f32[512]{0:T(512)S(1)}, f32[512]{0:T(512)S(1)}) fusion(f32[384,512]{1,0:T(8,128)S(1)} %copy-done.2, f32[384,512]{1,0:T(8,128)} %all-reduce.3.cloned.1.call-done, f32[384,512]{1,0:T(8,128)S(1)} %copy-done.1), kind=kLoop, calls=%fused_computation.4 | loop fusion | flops 1570816 | bytes 2367488 | tf_op jit(solution)/shard_map/reduce_sum | solution.py:49
  80.2 42.5 %all-reduce = (f32[512]{0:T(512)S(1)}, f32[512]{0:T(512)S(1)}, f32[512]{0:T(512)S(1)}, f32[512]{0:T(512)S(1)}) all-reduce(f32[512]{0:T(512)S(1)} %get-tuple-element.6, f32[512]{0:T(512)S(1)} %get-tuple-element.5, f32[512]{0:T(512)S(1)} %get-tuple-element.4, ...), channel_id=1, replica_groups=mesh['row'=2,'col'=8,'rep'=2] {'row','col'}, use_global_device_ids=true, to_apply=%region_1.0 | all-reduce | flops 2048 | bytes 16384 | tf_op jit(solution)/shard_map/psum | solution.py:45
  122.8 0.0 copy-done.3
  122.8 2.8 %multiply_add_fusion = (f32[384,512]{1,0:T(8,128)}, f32[384,512]{1,0:T(8,128)}, f32[384,512]{1,0:T(8,128)}) fusion(f32[384,512]{1,0:T(8,128)S(1)} %copy-done.1, f32[512]{0:T(512)S(1)} %get-tuple-element.13, f32[384,512]{1,0:T(8,128)S(1)} %copy-done.2, f32[384,512]{1,0:T(8,128)} %all-reduce.3.cloned.1.call-done, f32[512]{0:T(512)S(1)} %get-tuple-element.14, ...), kind=kLoop, calls=%fused_computation.2 | loop fusion | flops 1179648 | bytes 5509120 | tf_op jit(solution)/shard_map/add | solution.py:58
  (2 shorter events, 0.0 us)
Async XLA Ops:
  7.2 44.8 %copy-start = (f32[3,4,128,128]{3,2,1,0:T(8,128)S(1)}, f32[3,4,128,128]{3,2,1,0:T(8,128)}, u32[]{:S(2)}) copy-start(f32[3,4,128,128]{3,2,1,0:T(8,128)} %param.5) | copy-start | bytes 2359300
  7.2 71.6 %all-reduce.3.cloned.1.call-start = ((), (), s32[]{:S(2)}) async-start(), calls=%async_computation | async-start | bytes 1572864 | tf_op jit(solution)/shard_map/psum | solution.py:44
  7.2 39.6 %collective-permute-start.1 = (f32[384,512]{1,0:T(8,128)}, f32[384,512]{1,0:T(8,128)S(1)}, u32[]{:S(2)}, u32[]{:S(2)}) collective-permute-start(f32[384,512]{1,0:T(8,128)} %param.9), channel_id=1, source_target_pairs={{2,0},{4,2},{6,4},{8,6},{10,8},{12,10},{14,12},{16,14},{18,16},{20... | collective-permute-start | bytes 2359304 | tf_op jit(solution)/shard_map/ppermute | solution.py:20
  8.7 39.1 %collective-permute-start = (f32[384,512]{1,0:T(8,128)}, f32[384,512]{1,0:T(8,128)}, u32[]{:S(2)}, u32[]{:S(2)}) collective-permute-start(f32[384,512]{1,0:T(8,128)} %param.9), channel_id=1, source_target_pairs={{0,2},{2,4},{4,6},{6,8},{8,10},{10,12},{12,14},{14,16},{16,18},{18... | collective-permute-start | bytes 2359304 | tf_op jit(solution)/shard_map/ppermute | solution.py:17
  46.8 0.9 copy-start.4
  51.9 26.9 %copy-start.1 = (f32[384,512]{1,0:T(8,128)S(1)}, f32[384,512]{1,0:T(8,128)}, u32[]{:S(2)}) copy-start(f32[384,512]{1,0:T(8,128)} %param.9) | copy-start | bytes 2359300
  51.9 26.9 %copy-start.2 = (f32[384,512]{1,0:T(8,128)S(1)}, f32[384,512]{1,0:T(8,128)}, u32[]{:S(2)}) copy-start(f32[384,512]{1,0:T(8,128)} %param.8) | copy-start | bytes 2359300
  52.0 70.8 %copy-start.3 = (f32[384,512]{1,0:T(8,128)S(1)}, f32[384,512]{1,0:T(8,128)}, u32[]{:S(2)}) copy-start(f32[384,512]{1,0:T(8,128)} %param.7) | copy-start | bytes 2359300
Sparse Core Ops, SparseCore 0:
  56.9 21.8 all-reduce.2
where the time goes:
time: 133 us; the launch traced here: 132 us
  waiting for transfers between devices  53 us (40%)
  blocking collectives  42.5 us (32%)
  between operations  14.1 us (11%)
  starting transfers between devices  7.85 us (6%)
  other arithmetic  6.84 us (5%)
  matrix products  4.76 us (4%)
  local copies, waits for them, and re-layouts  3.4 us (3%)
    psum x1, blocking collectives, per_device(): lax.psum((jnp.sum(residual * residual, axis=0), jnp.sum(direction * image...  42.5 us
    ppermute x1, waiting for transfers between devices, extended_2(): lax.ppermute(lax.slice_in_dim(block, 0, width, axis=dim), axis, backward)  30.9 us
    psum x1, waiting for transfers between devices, per_device(): image = lax.psum(product.reshape(row_blocks * BLK, snapshots), 'rep')  22.1 us
    ppermute x1, starting transfers between devices, extended_2(): lax.ppermute(lax.slice_in_dim(block, block.shape[dim] - width, None, axis...  6.39 us
    dot_general x1, matrix products, per_device(): jnp.einsum('rkab,rkbs->ras', gain, picked, precision=lax.Precision.HIGHES...  4.76 us
    add x1, other arithmetic, per_device(): direction_next = residual_next + norm_new / norm_old * direction  2.82 us
  transfers between devices with their start and end apart: 3, of which 2 were waited for; matrix products, arithmetic and copies ran while one was open for 1% of the time, Pallas kernels for 0%

commit v1 on v0

v1 whole, which is shorter than its diff:
```python
import functools

import jax
import jax.numpy as jnp
from jax import lax
from jax.experimental import pallas as pl
from jax.experimental.pallas import tpu as pltpu
from jax.sharding import PartitionSpec as P

BLK = 128
LANES = 128
DIRECT_LIMIT = 16
CHUNK_ROWS = 64
MESH = pl.DeviceIdType.MESH


def split_bf16(value):
    high = value.astype(jnp.bfloat16)
    low = (value - high.astype(jnp.float32)).astype(jnp.bfloat16)
    return high, low


def iteration_kernel(
    sizes,
    columns_ref, gain_hbm, solution_hbm, residual_hbm, direction_hbm,
    solution_out, residual_out, direction_out,
    own_dir, own_res, own_sol, gains, near, far, band_high, band_low, images, totals, *rest,
):
    rows_n, cols_n = sizes
    segments = rows_n * cols_n
    direct = segments <= DIRECT_LIMIT
    phase_count = 1 if direct else 2
    parts = rest[:phase_count]
    part_send = rest[phase_count:2 * phase_count]
    part_recv = rest[2 * phase_count:3 * phase_count]
    (near_send, near_recv, far_send, far_recv, pair_send, pair_recv, local_sem) = rest[3 * phase_count:]

    seg_rows, half = near.shape
    block_rows = seg_rows // BLK
    slots_half = gains.shape[2]
    tiles = half // LANES
    chunks = seg_rows // CHUNK_ROWS

    row, col, rep = lax.axis_index("row"), lax.axis_index("col"), lax.axis_index("rep")
    seg = row * cols_n + col
    odd = lax.rem(seg, 2)
    other = 1 - rep

    def at_segment(index):
        return {"row": index // cols_n, "col": lax.rem(index, cols_n), "rep": rep}

    partner = {"row": row, "col": col, "rep": other}
    near_id = at_segment(seg + 1 - 2 * odd)
    target = seg + 2 - 4 * odd
    source = seg - 2 + 4 * odd
    sends_far = jnp.logical_and(target >= 0, target < segments)
    gets_far = jnp.logical_and(source >= 0, source < segments)
    far_id = at_segment(jnp.clip(target, 0, segments - 1))
    source_id = at_segment(jnp.clip(source, 0, segments - 1))

    if direct:
        phases = [(seg, segments, at_segment)]
    else:
        phases = [
            (col, cols_n, lambda index: {"row": row, "col": index, "rep": rep}),
            (row, rows_n, lambda index: {"row": index, "col": col, "rep": rep}),
        ]

    barrier = pltpu.get_barrier_semaphore()

    def greet(device):
        pl.semaphore_signal(barrier, inc=1, device_id=device, device_id_type=MESH)

    own_cols = pl.ds(pl.multiple_of(rep * half, LANES), half)
    other_cols = pl.ds(pl.multiple_of(other * half, LANES), half)
    load_dir = pltpu.make_async_copy(direction_hbm.at[:, own_cols], own_dir.at[:, own_cols], local_sem.at[0])
    load_gain = pltpu.make_async_copy(gain_hbm, gains.at[rep], local_sem.at[1])
    load_res = pltpu.make_async_copy(residual_hbm, own_res, local_sem.at[2])
    load_dir_other = pltpu.make_async_copy(direction_hbm.at[:, other_cols], own_dir.at[:, other_cols], local_sem.at[3])
    load_sol = pltpu.make_async_copy(solution_hbm, own_sol, local_sem.at[4])

    greet(partner)
    waits = 1
    if not direct:
        greet(near_id)
        waits += 1
    for place, count, device_of in phases:
        for step in range(1, count):
            greet(device_of(lax.rem(place + step, count)))
        waits += count - 1
    if not direct:
        @pl.when(sends_far)
        def _():
            greet(far_id)

        @pl.when(gets_far)
        def _():
            greet(source_id)

    load_dir.start()
    load_gain.start()
    load_res.start()
    load_dir_other.start()
    load_sol.start()

    pl.semaphore_wait(barrier, waits)
    if not direct:
        @pl.when(sends_far)
        def _():
            pl.semaphore_wait(barrier, 1)

        @pl.when(gets_far)
        def _():
            pl.semaphore_wait(barrier, 1)

    def near_copy(chunk):
        part = pl.ds(chunk * CHUNK_ROWS, CHUNK_ROWS)
        return pltpu.make_async_remote_copy(
            src_ref=own_dir.at[part, own_cols], dst_ref=near.at[part],
            send_sem=near_send.at[chunk], recv_sem=near_recv.at[chunk],
            device_id=near_id, device_id_type=MESH,
        )

    def far_copy(chunk):
        part = pl.ds(chunk * CHUNK_ROWS, CHUNK_ROWS)
        return pltpu.make_async_remote_copy(
            src_ref=near.at[part], dst_ref=far.at[part],
            send_sem=far_send.at[chunk], recv_sem=far_recv.at[chunk],
            device_id=far_id, device_id_type=MESH,
        )

    def pair_copy(index, src, dst):
        return pltpu.make_async_remote_copy(
            src_ref=src, dst_ref=dst, send_sem=pair_send.at[index], recv_sem=pair_recv.at[index],
            device_id=partner, device_id_type=MESH,
        )

    load_dir.wait()
    for chunk in range(chunks):
        near_copy(chunk).start()
    gain_pair = pair_copy(0, gain_hbm, gains.at[rep])
    gain_pair.start()

    first_block = seg * block_rows
    bases = (first_block, first_block + block_rows * (1 - 2 * odd), first_block - block_rows * (1 - 2 * odd))

    def build_band(group):
        for r in range(block_rows):
            names = [columns_ref[r, k] for k in range(2 * slots_half)]
            for j in range(block_rows):
                wanted = bases[group] + j
                slot = jnp.int32(0)
                found = jnp.float32(0)
                for k in reversed(range(2 * slots_half)):
                    match = names[k] == wanted
                    slot = jnp.where(match, k, slot)
                    found = jnp.where(match, jnp.float32(1), found)
                block = gains[slot // slots_half, r, lax.rem(slot, slots_half)] * found
                high, low = split_bf16(block)
                at = (group, pl.ds(r * BLK, BLK), pl.ds(j * BLK, BLK))
                band_high[at] = high
                band_low[at] = low

    def product(group, value):
        high, low = split_bf16(value)
        dot = functools.partial(jnp.dot, preferred_element_type=jnp.float32)
        return dot(band_high[group], high) + (dot(band_high[group], low) + dot(band_low[group], high))

    def tile_cols(side, tile):
        return pl.ds(pl.multiple_of(side * half + tile * LANES, LANES), LANES)

    def start_parts():
        load_res.wait()
        for tile in range(tiles):
            value = own_res[:, tile_cols(rep, tile)]
            parts[0][phases[0][0], pl.ds(tile, 1), :] = jnp.sum(value * value, axis=0, keepdims=True)

    def own_product():
        images[rep] = product(0, own_dir[:, own_cols])

    def gain_ready():
        load_gain.wait()
        gain_pair.wait()
        build_band(0)

    pieces = {0: start_parts, 1: gain_ready, 2: own_product, 3: lambda: build_band(1), 4: lambda: build_band(2)}
    for chunk in range(chunks):
        near_copy(chunk).wait_recv()

        @pl.when(sends_far)
        def _():
            far_copy(chunk).start()

        if chunk in pieces:
            pieces[chunk]()
    images[rep] += product(1, near[...])

    @pl.when(gets_far)
    def _():
        for chunk in range(chunks):
            far_copy(chunk).wait_recv()

    @pl.when(jnp.logical_not(gets_far))
    def _():
        far[...] = jnp.zeros_like(far)

    images[rep] += product(2, far[...])

    place0 = phases[0][0]
    for tile in range(tiles):
        image = images[rep, :, pl.ds(tile * LANES, LANES)]
        cols = tile_cols(rep, tile)
        for at, value in enumerate((own_dir[:, cols] * image, own_res[:, cols] * image, image * image)):
            parts[0][place0, pl.ds((at + 1) * tiles + tile, 1), :] = jnp.sum(value, axis=0, keepdims=True)

    image_pair = pair_copy(1, images.at[rep], images.at[rep])
    image_pair.start()

    for phase, (place, count, device_of) in enumerate(phases):
        copies = []
        for step in range(1, count):
            copies.append(pltpu.make_async_remote_copy(
                src_ref=parts[phase].at[place], dst_ref=parts[phase].at[place],
                send_sem=part_send[phase].at[step], recv_sem=part_recv[phase].at[step],
                device_id=device_of(lax.rem(place + step, count)), device_id_type=MESH,
            ))
        for copy in copies:
            copy.start()
        for copy in copies:
            copy.wait()
        total = parts[phase][0]
        for index in range(1, count):
            total = total + parts[phase][index]
        if phase + 1 < phase_count:
            parts[phase + 1][phases[phase + 1][0]] = total
        else:
            totals[rep] = total

    total_pair = pair_copy(2, totals.at[rep], totals.at[rep])
    total_pair.start()

    load_dir_other.wait()
    load_sol.wait()

    def update(side):
        for tile in range(tiles):
            norm_old, curvature, crossing, image_square = (
                totals[side, pl.ds(at * tiles + tile, 1), :] for at in range(4)
            )
            step_size = norm_old / curvature
            norm_new = norm_old - 2.0 * step_size * crossing + step_size * step_size * image_square
            scale = norm_new / norm_old
            cols = tile_cols(side, tile)
            direction = own_dir[:, cols]
            solution_out[:, cols] = own_sol[:, cols] + step_size * direction
            residual = own_res[:, cols] - step_size * images[side, :, pl.ds(tile * LANES, LANES)]
            residual_out[:, cols] = residual
            direction_out[:, cols] = residual + scale * direction

    update(rep)
    image_pair.wait()
    total_pair.wait()
    update(other)

    for chunk in range(chunks):
        near_copy(chunk).wait_send()

        @pl.when(sends_far)
        def _():
            far_copy(chunk).wait_send()


def solution(mesh):
    sizes = (mesh.shape["row"], mesh.shape["col"])
    segments = sizes[0] * sizes[1]
    counts = (segments,) if segments <= DIRECT_LIMIT else (sizes[1], sizes[0])

    def per_device(gain, coupled_columns, solution, residual, direction):
        seg_rows, snapshots = direction.shape
        half = snapshots // 2
        block_rows, slots_half = gain.shape[:2]
        chunks = seg_rows // CHUNK_ROWS
        sum_rows = 4 * (half // LANES)
        dma = pltpu.SemaphoreType.DMA
        whole = jax.ShapeDtypeStruct((seg_rows, snapshots), jnp.float32)
        any_space = pl.BlockSpec(memory_space=pl.ANY)
        vmem = pl.BlockSpec(memory_space=pltpu.VMEM)
        return pl.pallas_call(
            functools.partial(iteration_kernel, sizes),
            out_shape=(whole, whole, whole),
            in_specs=[pl.BlockSpec(memory_space=pltpu.SMEM), any_space, any_space, any_space, any_space],
            out_specs=(vmem, vmem, vmem),
            scratch_shapes=[
                pltpu.VMEM((seg_rows, snapshots), jnp.float32),
                pltpu.VMEM((seg_rows, snapshots), jnp.float32),
                pltpu.VMEM((seg_rows, snapshots), jnp.float32),
                pltpu.VMEM((2, block_rows, slots_half, BLK, BLK), jnp.float32),
                pltpu.VMEM((seg_rows, half), jnp.float32),
                pltpu.VMEM((seg_rows, half), jnp.float32),
                pltpu.VMEM((3, seg_rows, seg_rows), jnp.bfloat16),
                pltpu.VMEM((3, seg_rows, seg_rows), jnp.bfloat16),
                pltpu.VMEM((2, seg_rows, half), jnp.float32),
                pltpu.VMEM((2, sum_rows, LANES), jnp.float32),
                *[pltpu.VMEM((count, sum_rows, LANES), jnp.float32) for count in counts],
                *[dma((count,)) for count in counts],
                *[dma((count,)) for count in counts],
                dma((chunks,)), dma((chunks,)), dma((chunks,)), dma((chunks,)),
                dma((3,)), dma((3,)), dma((5,)),
            ],
            compiler_params=pltpu.CompilerParams(collective_id=0, has_side_effects=True),
            name="cg_iteration",
        )(coupled_columns, gain, solution, residual, direction)

    return jax.shard_map(
        per_device,
        mesh=mesh,
        in_specs=(
            P(("row", "col"), "rep", None, None),
            P(("row", "col"), None),
            P(("row", "col"), None),
            P(("row", "col"), None),
            P(("row", "col"), None),
        ),
        out_specs=(P(("row", "col"), None), P(("row", "col"), None), P(("row", "col"), None)),
        check_vma=False,
    )
```

time: 133 us -> 35.7 us (0.27)
  waiting for transfers between devices: 53 us -> 0 us
  blocking collectives: 42.5 us -> 0 us
  Pallas kernels: 0 us -> 30.4 us
  between operations: 14.1 us -> 0.65 us
  starting transfers between devices: 7.85 us -> 0 us
  other arithmetic: 6.84 us -> 0 us
  matrix products: 4.76 us -> 0 us
    psum x1 -> x0, blocking collectives: 42.5 us -> none  [per_device(): lax.psum((jnp.sum(residual * residual, axis=0), jnp.sum(direction * image...]
    ppermute x2 -> x0, waiting for transfers between devices: 30.9 us -> none  [the longest x1 30.9 us: extended_2(): lax.ppermute(lax.slice_in_dim(block, 0, width, axis=dim), axis, backward)]
    pallas_call x0 -> x1, Pallas kernels: none -> 30.4 us  [per_device(): pl.pallas_call(functools.partial(iteration_kernel, sizes), out_shape=(who...]
    psum x1 -> x0, waiting for transfers between devices: 22.1 us -> none  [per_device(): image = lax.psum(product.reshape(row_blocks * BLK, snapshots), 'rep')]
    ppermute x2 -> x0, starting transfers between devices: 7.81 us -> none  [the longest x1 6.39 us: extended_2(): lax.ppermute(lax.slice_in_dim(block, block.shape[dim] - width, None, axis...]
    dot_general x1 -> x0, matrix products: 4.76 us -> none  [per_device(): jnp.einsum('rkab,rkbs->ras', gain, picked, precision=lax.Precision.HIGHES...]
    unnamed x10 -> x7, local copies, waits for them, and re-layouts: 0.9 us -> 4.44 us
    add x1 -> x0, other arithmetic: 2.82 us -> none  [per_device(): direction_next = residual_next + norm_new / norm_old * direction]
  transfers between devices with their start and end apart: 3 -> 0, of which waited for: 2 -> 0; matrix products, arithmetic and copies ran while one was open for 1% -> 0% of each run, Pallas kernels for 0% -> 0%
where the time goes in v1:
time: 35.7 us; the launch traced here: 35.5 us
  Pallas kernels  30.4 us (85%)
  local copies, waits for them, and re-layouts  4.44 us (12%)
  between operations  0.65 us (2%)
    pallas_call x1, Pallas kernels, per_device(): pl.pallas_call(functools.partial(iteration_kernel, sizes), out_shape=(who...  30.4 us
    unnamed x7, local copies, waits for them, and re-layouts  4.44 us

profile of v1, /device:TPU:0, one launch (start us, length us, event | category | flops | bytes accessed | tf_op | source)
XLA Modules:
  0.0 35.5 jit_solution(12491411273007089090)
XLA Ops:
  0.6 30.4 %cg_iteration.1 = (f32[384,512]{1,0:T(8,128)}, f32[384,512]{1,0:T(8,128)}, f32[384,512]{1,0:T(8,128)}) custom-call(s32[3,8]{1,0:T(4,128)} %columns_ref.1, f32[3,4,128,128]{3,2,1,0:T(8,128)} %gain_hbm.1, f32[384,512]{1,0:T(8,128)} %solution_hbm.1, f32[384,512]{1,0:T(8,128)} %residual_hbm.1, f32[384,512]{1,0:T(8,128)} %direction_hbm.1), custom_call_target="tpu_custom_call" | custom-call | tf_op jit(solution)/shard_map/cg_iteration/pallas_call | solution.py:288
  31.1 0.0 copy-start.1
  31.1 2.1 %copy.11 = f32[384,512]{1,0:T(8,128)} copy(f32[384,512]{1,0:T(8,128)} %get-tuple-element.6) | data formatting | bytes 1572864
  33.2 0.0 copy-done.1
  33.2 0.0 copy-start
  33.2 0.9 %copy.12 = f32[384,512]{1,0:T(8,128)} copy(f32[384,512]{1,0:T(8,128)S(1)} %copy-done.1) | data formatting | bytes 1572864
  34.1 0.5 %copy-done = f32[384,512]{1,0:T(8,128)S(1)} copy-done((f32[384,512]{1,0:T(8,128)S(1)}, f32[384,512]{1,0:T(8,128)}, u32[]{:S(2)}) %copy-start) | copy-done | bytes 786456
  34.6 0.9 %copy.13 = f32[384,512]{1,0:T(8,128)} copy(f32[384,512]{1,0:T(8,128)S(1)} %copy-done) | data formatting | bytes 1572864
Async XLA Ops:
  31.1 2.1 %copy-start.1 = (f32[384,512]{1,0:T(8,128)S(1)}, f32[384,512]{1,0:T(8,128)}, u32[]{:S(2)}) copy-start(f32[384,512]{1,0:T(8,128)} %get-tuple-element.7) | copy-start | bytes 2359300
  33.2 1.4 %copy-start = (f32[384,512]{1,0:T(8,128)S(1)}, f32[384,512]{1,0:T(8,128)}, u32[]{:S(2)}) copy-start(f32[384,512]{1,0:T(8,128)} %get-tuple-element.8) | copy-start | bytes 2359300

commit v2 on v1

--- a/solution.py
+++ b/solution.py
@@ -10,7 +10,7 @@
 BLK = 128
 LANES = 128
 DIRECT_LIMIT = 16
-CHUNK_ROWS = 64
+CHUNK_ROWS = 32
 MESH = pl.DeviceIdType.MESH
 
 
@@ -23,8 +23,8 @@
 def iteration_kernel(
     sizes,
     columns_ref, gain_hbm, solution_hbm, residual_hbm, direction_hbm,
-    solution_out, residual_out, direction_out,
-    own_dir, own_res, own_sol, gains, near, far, band_high, band_low, images, totals, *rest,
+    own_dir, own_res, own_sol, images, steps, scales,
+    gains, near, far, band_high, band_low, totals, *rest,
 ):
     rows_n, cols_n = sizes
     segments = rows_n * cols_n
@@ -176,7 +176,7 @@
             parts[0][phases[0][0], pl.ds(tile, 1), :] = jnp.sum(value * value, axis=0, keepdims=True)
 
     def own_product():
-        images[rep] = product(0, own_dir[:, own_cols])
+        images[:, own_cols] = product(0, own_dir[:, own_cols])
 
     def gain_ready():
         load_gain.wait()
@@ -193,7 +193,7 @@
 
         if chunk in pieces:
             pieces[chunk]()
-    images[rep] += product(1, near[...])
+    images[:, own_cols] += product(1, near[...])
 
     @pl.when(gets_far)
     def _():
@@ -204,16 +204,16 @@
     def _():
         far[...] = jnp.zeros_like(far)
 
-    images[rep] += product(2, far[...])
+    images[:, own_cols] += product(2, far[...])
 
     place0 = phases[0][0]
     for tile in range(tiles):
-        image = images[rep, :, pl.ds(tile * LANES, LANES)]
         cols = tile_cols(rep, tile)
+        image = images[:, cols]
         for at, value in enumerate((own_dir[:, cols] * image, own_res[:, cols] * image, image * image)):
             parts[0][place0, pl.ds((at + 1) * tiles + tile, 1), :] = jnp.sum(value, axis=0, keepdims=True)
 
-    image_pair = pair_copy(1, images.at[rep], images.at[rep])
+    image_pair = pair_copy(1, images.at[:, own_cols], images.at[:, own_cols])
     image_pair.start()
 
     for phase, (place, count, device_of) in enumerate(phases):
@@ -242,25 +242,21 @@
     load_dir_other.wait()
     load_sol.wait()
 
-    def update(side):
+    def make_factors(side):
         for tile in range(tiles):
             norm_old, curvature, crossing, image_square = (
                 totals[side, pl.ds(at * tiles + tile, 1), :] for at in range(4)
             )
             step_size = norm_old / curvature
             norm_new = norm_old - 2.0 * step_size * crossing + step_size * step_size * image_square
-            scale = norm_new / norm_old
             cols = tile_cols(side, tile)
-            direction = own_dir[:, cols]
-            solution_out[:, cols] = own_sol[:, cols] + step_size * direction
-            residual = own_res[:, cols] - step_size * images[side, :, pl.ds(tile * LANES, LANES)]
-            residual_out[:, cols] = residual
-            direction_out[:, cols] = residual + scale * direction
-
-    update(rep)
+            steps[:, cols] = step_size
+            scales[:, cols] = norm_new / norm_old
+
+    make_factors(rep)
     image_pair.wait()
     total_pair.wait()
-    update(other)
+    make_factors(other)
 
     for chunk in range(chunks):
         near_copy(chunk).wait_send()
@@ -282,24 +278,21 @@
         chunks = seg_rows // CHUNK_ROWS
         sum_rows = 4 * (half // LANES)
         dma = pltpu.SemaphoreType.DMA
-        whole = jax.ShapeDtypeStruct((seg_rows, snapshots), jnp.float32)
+        whole = pltpu.VMEM((seg_rows, snapshots), jnp.float32)
+        line = pltpu.VMEM((1, snapshots), jnp.float32)
         any_space = pl.BlockSpec(memory_space=pl.ANY)
         vmem = pl.BlockSpec(memory_space=pltpu.VMEM)
-        return pl.pallas_call(
+        held, residual_held, solution_held, image, steps, scales = pl.pallas_call(
             functools.partial(iteration_kernel, sizes),
-            out_shape=(whole, whole, whole),
+            out_shape=(whole, whole, whole, whole, line, line),
             in_specs=[pl.BlockSpec(memory_space=pltpu.SMEM), any_space, any_space, any_space, any_space],
-            out_specs=(vmem, vmem, vmem),
+            out_specs=(vmem,) * 6,
             scratch_shapes=[
-                pltpu.VMEM((seg_rows, snapshots), jnp.float32),
-                pltpu.VMEM((seg_rows, snapshots), jnp.float32),
-                pltpu.VMEM((seg_rows, snapshots), jnp.float32),
                 pltpu.VMEM((2, block_rows, slots_half, BLK, BLK), jnp.float32),
                 pltpu.VMEM((seg_rows, half), jnp.float32),
                 pltpu.VMEM((seg_rows, half), jnp.float32),
                 pltpu.VMEM((3, seg_rows, seg_rows), jnp.bfloat16),
                 pltpu.VMEM((3, seg_rows, seg_rows), jnp.bfloat16),
-                pltpu.VMEM((2, seg_rows, half), jnp.float32),
                 pltpu.VMEM((2, sum_rows, LANES), jnp.float32),
                 *[pltpu.VMEM((count, sum_rows, LANES), jnp.float32) for count in counts],
                 *[dma((count,)) for count in counts],
@@ -310,6 +303,8 @@
             compiler_params=pltpu.CompilerParams(collective_id=0, has_side_effects=True),
             name="cg_iteration",
         )(coupled_columns, gain, solution, residual, direction)
+        residual_next = residual_held - steps * image
+        return solution_held + steps * held, residual_next, residual_next + scales * held
 
     return jax.shard_map(
         per_device,

time: 35.7 us -> 31 us (0.87)
  local copies, waits for them, and re-layouts: 4.44 us -> 0 us
  Pallas kernels: 30.4 us -> 28.5 us
  other arithmetic: 0 us -> 1.68 us
    unnamed x7 -> x0, local copies, waits for them, and re-layouts: 4.44 us -> none
    pallas_call x1, Pallas kernels: 30.4 us -> 28.5 us  [per_device(): pl.pallas_call(functools.partial(iteration_kernel, sizes), out_shape=(who...]
    add x0 -> x1, other arithmetic: none -> 1.68 us  [per_device(): residual_next + scales * held]
where the time goes in v2:
time: 31 us; the launch traced here: 30.8 us
  Pallas kernels  28.5 us (92%)
  other arithmetic  1.68 us (5%)
  between operations  0.64 us (2%)
    pallas_call x1, Pallas kernels, per_device(): pl.pallas_call(functools.partial(iteration_kernel, sizes), out_shape=(who...  28.5 us
    add x1, other arithmetic, per_device(): residual_next + scales * held  1.68 us

profile of v2, /device:TPU:0, one launch (start us, length us, event | category | flops | bytes accessed | tf_op | source)
XLA Modules:
  0.0 30.8 jit_solution(17206466735844975903)
XLA Ops:
  0.6 28.5 %cg_iteration.1 = (f32[384,512]{1,0:T(8,128)S(1)}, f32[384,512]{1,0:T(8,128)S(1)}, f32[384,512]{1,0:T(8,128)S(1)}, f32[384,512]{1,0:T(8,128)S(1)}, f32[1,512]{1,0:T(1,128)S(1)}, /*index=5*/f32[1,512]{1,0:T(1,128)S(1)}) custom-call(s32[3,8]{1,0:T(4,128)} %columns_ref.1, f32[3,4,128,128]{3,2,1,0:T(8,128)} %gain_hbm.1, f32[384,512]{1,0:T(8,128)} %solution_hbm.1, ...), custom_call_target="tpu_custom_call" | custom-call | tf_op jit(solution)/shard_map/cg_iteration/pallas_call | solution.py:285
  29.1 1.7 %multiply_add_fusion = (f32[384,512]{1,0:T(8,128)}, f32[384,512]{1,0:T(8,128)}, f32[384,512]{1,0:T(8,128)}) fusion(f32[384,512]{1,0:T(8,128)S(1)} %get-tuple-element.11, f32[512]{0:T(512)S(1)} %bitcast.3, f32[384,512]{1,0:T(8,128)S(1)} %get-tuple-element.12, f32[384,512]{1,0:T(8,128)S(1)} %get-tuple-element.13, f32[512]{0:T(512)S(1)} %bitcast.2, ...), kind=kLoop, calls=%fused_computation | loop fusion | flops 1179648 | bytes 5509120 | tf_op jit(solution)/shard_map/add | solution.py:307

commit v3 on v2

--- a/solution.py
+++ b/solution.py
@@ -33,7 +33,7 @@
     parts = rest[:phase_count]
     part_send = rest[phase_count:2 * phase_count]
     part_recv = rest[2 * phase_count:3 * phase_count]
-    (near_send, near_recv, far_send, far_recv, pair_send, pair_recv, local_sem) = rest[3 * phase_count:]
+    (near_send, near_recv, far_send, far_recv, pair_send, pair_recv, local_sem, known) = rest[3 * phase_count:]
 
     seg_rows, half = near.shape
     block_rows = seg_rows // BLK
@@ -80,15 +80,30 @@
     load_sol = pltpu.make_async_copy(solution_hbm, own_sol, local_sem.at[4])
 
     greet(partner)
-    waits = 1
-    if not direct:
+    if direct:
+        steps_around = [
+            (jnp.bool_(True), {"row": row, "col": col + 1 - 2 * odd, "rep": rep}),
+            (col >= 2, {"row": row, "col": jnp.maximum(col - 2, 0), "rep": rep}),
+            (col + 2 < cols_n, {"row": row, "col": jnp.minimum(col + 2, cols_n - 1), "rep": rep}),
+            (row >= 1, {"row": jnp.maximum(row - 1, 0), "col": col, "rep": rep}),
+            (row + 1 < rows_n, {"row": jnp.minimum(row + 1, rows_n - 1), "col": col, "rep": rep}),
+        ]
+
+        near_count = sum(exists.astype(jnp.int32) for exists, device in steps_around)
+
+        def around(act):
+            for exists, device in steps_around:
+                @pl.when(exists)
+                def _(device=device):
+                    act(device)
+
+        around(greet)
+    else:
         greet(near_id)
-        waits += 1
-    for place, count, device_of in phases:
-        for step in range(1, count):
-            greet(device_of(lax.rem(place + step, count)))
-        waits += count - 1
-    if not direct:
+        for place, count, device_of in phases:
+            for step in range(1, count):
+                greet(device_of(lax.rem(place + step, count)))
+
         @pl.when(sends_far)
         def _():
             greet(far_id)
@@ -103,8 +118,11 @@
     load_dir_other.start()
     load_sol.start()
 
-    pl.semaphore_wait(barrier, waits)
-    if not direct:
+    if direct:
+        pl.semaphore_wait(barrier, 1 + near_count)
+    else:
+        pl.semaphore_wait(barrier, 2 + sum(count - 1 for place, count, device_of in phases))
+
         @pl.when(sends_far)
         def _():
             pl.semaphore_wait(barrier, 1)
@@ -112,6 +130,13 @@
         @pl.when(gets_far)
         def _():
             pl.semaphore_wait(barrier, 1)
+
+    def spread(step):
+        around(lambda device: pl.semaphore_signal(
+            known.at[step], inc=1, device_id=device, device_id_type=MESH))
+
+    def learn(step):
+        pl.semaphore_wait(known.at[step], near_count)
 
     def near_copy(chunk):
         part = pl.ds(chunk * CHUNK_ROWS, CHUNK_ROWS)
@@ -140,6 +165,12 @@
         near_copy(chunk).start()
     gain_pair = pair_copy(0, gain_hbm, gains.at[rep])
     gain_pair.start()
+
+    rounds = rows_n + cols_n // 2 - 2 if direct else 0
+    for step in range(rounds):
+        spread(step)
+        if step < rounds - 1:
+            learn(step)
 
     first_block = seg * block_rows
     bases = (first_block, first_block + block_rows * (1 - 2 * odd), first_block - block_rows * (1 - 2 * odd))
@@ -206,6 +237,8 @@
 
     images[:, own_cols] += product(2, far[...])
 
+    if rounds:
+        learn(rounds - 1)
     place0 = phases[0][0]
     for tile in range(tiles):
         cols = tile_cols(rep, tile)
@@ -269,6 +302,7 @@
 def solution(mesh):
     sizes = (mesh.shape["row"], mesh.shape["col"])
     segments = sizes[0] * sizes[1]
+    rounds = max(sizes[0] + sizes[1] // 2 - 2, 1)
     counts = (segments,) if segments <= DIRECT_LIMIT else (sizes[1], sizes[0])
 
     def per_device(gain, coupled_columns, solution, residual, direction):
@@ -298,7 +332,7 @@
                 *[dma((count,)) for count in counts],
                 *[dma((count,)) for count in counts],
                 dma((chunks,)), dma((chunks,)), dma((chunks,)), dma((chunks,)),
-                dma((3,)), dma((3,)), dma((5,)),
+                dma((3,)), dma((3,)), dma((5,)), pltpu.SemaphoreType.REGULAR((rounds,)),
             ],
             compiler_params=pltpu.CompilerParams(collective_id=0, has_side_effects=True),
             name="cg_iteration",

time: 31 us -> 29 us (0.935)
  Pallas kernels: 28.5 us -> 26.5 us
    pallas_call x1, Pallas kernels: 28.5 us -> 26.5 us  [per_device(): pl.pallas_call(functools.partial(iteration_kernel, sizes), out_shape=(who...]
where the time goes in v3:
time: 29 us; the launch traced here: 28.9 us
  Pallas kernels  26.5 us (91%)
  other arithmetic  1.68 us (6%)
  between operations  0.64 us (2%)
    pallas_call x1, Pallas kernels, per_device(): pl.pallas_call(functools.partial(iteration_kernel, sizes), out_shape=(who...  26.5 us
    add x1, other arithmetic, per_device(): residual_next + scales * held  1.68 us

profile of v3, /device:TPU:0, one launch (start us, length us, event | category | flops | bytes accessed | tf_op | source)
XLA Modules:
  0.0 28.9 jit_solution(14125312071265336476)
XLA Ops:
  0.6 26.5 %cg_iteration.1 = (f32[384,512]{1,0:T(8,128)S(1)}, f32[384,512]{1,0:T(8,128)S(1)}, f32[384,512]{1,0:T(8,128)S(1)}, f32[384,512]{1,0:T(8,128)S(1)}, f32[1,512]{1,0:T(1,128)S(1)}, /*index=5*/f32[1,512]{1,0:T(1,128)S(1)}) custom-call(s32[3,8]{1,0:T(4,128)} %columns_ref.1, f32[3,4,128,128]{3,2,1,0:T(8,128)} %gain_hbm.1, f32[384,512]{1,0:T(8,128)} %solution_hbm.1, ...), custom_call_target="tpu_custom_call" | custom-call | tf_op jit(solution)/shard_map/cg_iteration/pallas_call | solution.py:319
  27.2 1.7 %multiply_add_fusion = (f32[384,512]{1,0:T(8,128)}, f32[384,512]{1,0:T(8,128)}, f32[384,512]{1,0:T(8,128)}) fusion(f32[384,512]{1,0:T(8,128)S(1)} %get-tuple-element.11, f32[512]{0:T(512)S(1)} %bitcast.3, f32[384,512]{1,0:T(8,128)S(1)} %get-tuple-element.12, f32[384,512]{1,0:T(8,128)S(1)} %get-tuple-element.13, f32[512]{0:T(512)S(1)} %bitcast.2, ...), kind=kLoop, calls=%fused_computation | loop fusion | flops 1179648 | bytes 5509120 | tf_op jit(solution)/shard_map/add | solution.py:341

commit v4 on v3

--- a/solution.py
+++ b/solution.py
@@ -10,7 +10,7 @@
 BLK = 128
 LANES = 128
 DIRECT_LIMIT = 16
-CHUNK_ROWS = 32
+CHUNK_ROWS = 64
 MESH = pl.DeviceIdType.MESH
 
 
@@ -257,7 +257,7 @@
                 send_sem=part_send[phase].at[step], recv_sem=part_recv[phase].at[step],
                 device_id=device_of(lax.rem(place + step, count)), device_id_type=MESH,
             ))
-        for copy in copies:
+        for copy in reversed(copies):
             copy.start()
         for copy in copies:
             copy.wait()

time: 29 us -> 29.1 us (level)
  no operation moved by 1% of the time
where the time goes in v4:
time: 29.1 us; the launch traced here: 29 us
  Pallas kernels  26.7 us (92%)
  other arithmetic  1.68 us (6%)
  between operations  0.64 us (2%)
    pallas_call x1, Pallas kernels, per_device(): pl.pallas_call(functools.partial(iteration_kernel, sizes), out_shape=(who...  26.7 us
    add x1, other arithmetic, per_device(): residual_next + scales * held  1.68 us

profile of v4, /device:TPU:0, one launch (start us, length us, event | category | flops | bytes accessed | tf_op | source)
XLA Modules:
  0.0 29.0 jit_solution(15235629411965320964)
XLA Ops:
  0.6 26.7 %cg_iteration.1 = (f32[384,512]{1,0:T(8,128)S(1)}, f32[384,512]{1,0:T(8,128)S(1)}, f32[384,512]{1,0:T(8,128)S(1)}, f32[384,512]{1,0:T(8,128)S(1)}, f32[1,512]{1,0:T(1,128)S(1)}, /*index=5*/f32[1,512]{1,0:T(1,128)S(1)}) custom-call(s32[3,8]{1,0:T(4,128)} %columns_ref.1, f32[3,4,128,128]{3,2,1,0:T(8,128)} %gain_hbm.1, f32[384,512]{1,0:T(8,128)} %solution_hbm.1, ...), custom_call_target="tpu_custom_call" | custom-call | tf_op jit(solution)/shard_map/cg_iteration/pallas_call | solution.py:319
  27.3 1.7 %multiply_add_fusion = (f32[384,512]{1,0:T(8,128)}, f32[384,512]{1,0:T(8,128)}, f32[384,512]{1,0:T(8,128)}) fusion(f32[384,512]{1,0:T(8,128)S(1)} %get-tuple-element.11, f32[512]{0:T(512)S(1)} %bitcast.3, f32[384,512]{1,0:T(8,128)S(1)} %get-tuple-element.12, f32[384,512]{1,0:T(8,128)S(1)} %get-tuple-element.13, f32[512]{0:T(512)S(1)} %bitcast.2, ...), kind=kLoop, calls=%fused_computation | loop fusion | flops 1179648 | bytes 5509120 | tf_op jit(solution)/shard_map/add | solution.py:341
